TPU v7x, 256 devices: a whole 4x4x8 slice. The times are simulated.
256 devices in a mesh: dp: 32 (over z, x_hi, core), expert: 8 (over x_lo, y).
Axes of the slice: x: 4 (x_hi: 2, x_lo: 2; x = x_hi * 2 + x_lo), y: 4, z: 8, core: 2. Of those that a mesh axis runs over, the one named last changes fastest.
Arguments:
- x_rows: bfloat16 [131072, 1024], P(('dp', 'expert')), may hold values from -24 to 24
- dy_rows: bfloat16 [131072, 2048], P(('dp', 'expert')), may hold values from -0.0234375 to 0.0234375
- seg_blocks: int32 [256, 8], replicated, may hold values from 0 to 2, as said below
Outputs:
- expert_grad: float32 [8, 1024, 2048], P(None, 'dp', 'expert')
Inputs may be any that keep to these rules, and one draw needn't show every extreme that they name: `seg_blocks`: on every device the entries sum to at most 4; one expert has exactly 2 blocks on every device.
All inputs are finite; a program needn't handle non-finite values.
Results may differ from a plain program's by a relative error of at most 0.0003.
Values may be sent and summed in bfloat16 or wider, within the bound.
A program may use at most 128 MiB of HBM per device.

v0:
```python
import jax
import jax.numpy as jnp
from jax import lax
from jax.sharding import PartitionSpec as P

BLOCK = 128


def row_owners(seg_blocks, devices, nblk):
    counts = seg_blocks[devices]
    ends = jnp.cumsum(counts, axis=1)
    block = jnp.arange(nblk, dtype=jnp.int32)
    return jnp.sum((ends[:, None, :] <= block[None, :, None]).astype(jnp.int32), axis=2)


def shards(x_rows, dy_rows, seg_blocks):
    rows, hid = x_rows.shape
    ffn = dy_rows.shape[1]
    n_exp = lax.axis_size("expert")
    experts = seg_blocks.shape[1]
    nblk = rows // BLOCK
    devices = lax.axis_index("dp") * n_exp + jnp.arange(n_exp)
    owner = row_owners(seg_blocks, devices, nblk).reshape(-1)
    mask = (owner[None, :] == jnp.arange(experts)[:, None]).astype(x_rows.dtype)
    mask = jnp.repeat(mask, BLOCK, axis=1)
    xg = lax.all_gather(x_rows, "expert", axis=0, tiled=True)
    dyg = lax.all_to_all(dy_rows, "expert", split_axis=1, concat_axis=0, tiled=True)
    xm = xg[None] * mask[:, :, None]
    part = jnp.einsum("eth,tf->ehf", xm, dyg, preferred_element_type=jnp.float32)
    return lax.psum_scatter(part, "dp", scatter_dimension=1, tiled=True)


def solution(mesh):
    in_specs = (P(("dp", "expert"), None), P(("dp", "expert"), None), P())
    out_specs = P(None, "dp", "expert")
    return jax.shard_map(shards, mesh=mesh, in_specs=in_specs, out_specs=out_specs, check_vma=False)
```

profile of v0, /device:TPU:8, one launch (start us, length us, event | category | flops | bytes accessed | tf_op | source)
XLA Modules:
  0.0 318.6 jit_solution(7816214932795877325)
XLA Ops:
  6.5 0.0 copy-start
  6.5 0.0 all-gather.2.cloned.1.call-start
  6.5 0.7 all-gather.2.cloned.1.call-update
  7.3 3.1 copy.16
  10.3 5.8 %all-to-all-start = ((bf16[512,8,256]{2,0,1:T(8,128)(2,1)}), bf16[512,8,256]{2,0,1:T(8,128)(2,1)S(1)}, u32[]{:S(2)}, u32[]{:S(2)}) async-start(bf16[512,8,256]{2,0,1:T(8,128)(2,1)} %bitcast.13), calls=%async_computation | async-start | bytes 4194304 | tf_op jit(solution)/shard_map/all_to_all | solution.py:27
  16.2 0.0 reduce-scatter.2.cloned.1.call-start
  16.2 0.0 copy-done
  16.2 0.1 copy.11
  16.3 0.6 gather_fusion
  16.9 0.2 reduce_window_sum.11
  17.1 0.1 convert_reduce_fusion
  17.2 0.1 copy.12
  17.3 0.1 eq.15
  17.4 0.1 fusion.4
  17.4 0.1 broadcast_bitcast_fusion
  17.6 102.1 %all-gather.2.cloned.1.call-done = bf16[4096,1024]{1,0:T(8,128)(2,1)} async-done(((bf16[512,1024]{1,0:T(8,128)(2,1)}), bf16[4096,1024]{1,0:T(8,128)(2,1)}) %all-gather.2.cloned.1.call-update) | async-done | bytes 8388624 | tf_op jit(solution)/shard_map/all_gather | solution.py:26
  119.6 11.8 %copy.10 = bf16[4096,1024]{0,1:T(8,128)(2,1)} copy(bf16[4096,1024]{1,0:T(8,128)(2,1)} %all-gather.2.cloned.1.call-done) | data formatting | bytes 16777216 | tf_op jit(solution)/shard_map/all_gather | solution.py:26
  131.4 0.0 all-to-all-done
  131.4 22.7 %fusion = f32[8,1024,256]{2,1,0:T(8,128)} fusion(bf16[4096,256,1]{1,0,2:T(8,128)(2,1)S(1)} %bitcast.15, bf16[8,4096]{1,0:T(8,128)(2,1)S(1)} %broadcast_bitcast_fusion, bf16[4096,1024]{0,1:T(8,128)(2,1)} %copy.10), kind=kOutput, calls=%fused_computation.1 | convolution fusion | flops 17213423616 | bytes 18939904 | tf_op jit(solution)/shard_map/eth,tf->ehf/dot_general | solution.py:29
  154.2 0.0 reduce-scatter.2.cloned.1.call-update
  154.2 157.6 %reduce-scatter.2.cloned.1.call-done = f32[8,32,256]{2,1,0:T(8,128)} async-done(((f32[8,1024,256]{2,1,0:T(8,128)}), f32[8,32,256]{2,1,0:T(8,128)}) %reduce-scatter.2.cloned.1.call-update) | async-done | bytes 262160 | tf_op jit(solution)/shard_map/reduce_scatter | solution.py:30
  (2 shorter events, 0.0 us)
Async XLA Ops:
  6.5 9.6 %copy-start = (s32[256,8]{0,1:T(8,128)S(1)}, s32[256,8]{0,1:T(8,128)}, u32[]{:S(2)}) copy-start(s32[256,8]{0,1:T(8,128)} %param.5) | copy-start | bytes 24580
  6.5 113.1 %all-gather.2.cloned.1.call-start = ((), (), s32[]{:S(2)}) async-start(), calls=%async_computation.2 | async-start | bytes 9437184 | tf_op jit(solution)/shard_map/all_gather | solution.py:26
  10.3 121.1 %all-to-all-start = ((bf16[512,8,256]{2,0,1:T(8,128)(2,1)}), bf16[512,8,256]{2,0,1:T(8,128)(2,1)S(1)}, u32[]{:S(2)}, u32[]{:S(2)}) async-start(bf16[512,8,256]{2,0,1:T(8,128)(2,1)} %bitcast.13), calls=%async_computation | async-start | bytes 4194304 | tf_op jit(solution)/shard_map/all_to_all | solution.py:27
  16.2 295.6 %reduce-scatter.2.cloned.1.call-start = ((), (), s32[]{:S(2)}) async-start(), calls=%async_computation.3 | async-start | bytes 8650752 | tf_op jit(solution)/shard_map/reduce_scatter | solution.py:30
Sparse Core Ops, SparseCore 0:
  9.1 110.4 all-gather.1
  154.3 157.4 reduce-scatter.1
where the time goes:
time: 319 us
  waiting for transfers between devices  260 us (82%)
  matrix products  22.7 us (7%)
  local copies, waits for them, and re-layouts  15.8 us (5%)
  between operations  13.4 us (4%)
  starting transfers between devices  5.85 us (2%)
    reduce_scatter x1, waiting for transfers between devices, shards(): return lax.psum_scatter(part, 'dp', scatter_dimension=1, tiled=True)  158 us
    all_gather x1, waiting for transfers between devices, shards(): xg = lax.all_gather(x_rows, 'expert', axis=0, tiled=True)  102 us
    dot_general x1, matrix products, shards(): jnp.einsum('eth,tf->ehf', xm, dyg, preferred_element_type=jnp.float32)  22.7 us
    all_gather x1, local copies, waits for them, and re-layouts, shards(): xg = lax.all_gather(x_rows, 'expert', axis=0, tiled=True)  11.8 us
  transfers between devices with their start and end apart: 3, of which 2 were waited for; matrix products, arithmetic and copies ran while one was open for 5% of the time, Pallas kernels for 0%

commit v1 on v0

--- a/solution.py
+++ b/solution.py
@@ -23,7 +23,8 @@
     owner = row_owners(seg_blocks, devices, nblk).reshape(-1)
     mask = (owner[None, :] == jnp.arange(experts)[:, None]).astype(x_rows.dtype)
     mask = jnp.repeat(mask, BLOCK, axis=1)
-    xg = lax.all_gather(x_rows, "expert", axis=0, tiled=True)
+    outgoing = jnp.stack([x_rows] * lax.axis_size("expert"))
+    xg = jnp.concatenate(lax.all_to_all(outgoing, "expert", 0, 0), axis=0)
     dyg = lax.all_to_all(dy_rows, "expert", split_axis=1, concat_axis=0, tiled=True)
     xm = xg[None] * mask[:, :, None]
     part = jnp.einsum("eth,tf->ehf", xm, dyg, preferred_element_type=jnp.float32)

time: 319 us -> 327 us (1.025)
  local copies, waits for them, and re-layouts: 15.8 us -> 31.1 us
  waiting for transfers between devices: 260 us -> 247 us
  starting transfers between devices: 5.85 us -> 11.9 us
    all_gather x1 -> x0, waiting for transfers between devices: 102 us -> none  [shards(): xg = lax.all_gather(x_rows, 'expert', axis=0, tiled=True)]
    all_to_all x0 -> x1, waiting for transfers between devices: none -> 89.8 us  [shards(): xg = jnp.concatenate(lax.all_to_all(outgoing, 'expert', 0, 0), axis=0)]
    all_gather x1 -> x0, local copies, waits for them, and re-layouts: 11.8 us -> none  [shards(): xg = lax.all_gather(x_rows, 'expert', axis=0, tiled=True)]
    mul x1 -> x2, local copies, waits for them, and re-layouts: 0.11 us -> 11.9 us  [shards(): xm = xg[None] * mask[:, :, None]]
    all_to_all x0 -> x1, local copies, waits for them, and re-layouts: none -> 11.4 us  [shards(): xg = jnp.concatenate(lax.all_to_all(outgoing, 'expert', 0, 0), axis=0)]
    all_to_all x0 -> x1, starting transfers between devices: none -> 7.12 us  [shards(): xg = jnp.concatenate(lax.all_to_all(outgoing, 'expert', 0, 0), axis=0)]
    another operation x0 -> x1, local copies, waits for them, and re-layouts: none -> 3.93 us  [shards(): outgoing = jnp.stack([x_rows] * lax.axis_size('expert'))]
  transfers between devices with their start and end apart: 3 -> 3, of which waited for: 2 -> 3; matrix products, arithmetic and copies ran while one was open for 5% -> 8% of each run, Pallas kernels for 0% -> 0%
where the time goes in v1:
time: 327 us
  waiting for transfers between devices  247 us (76%)
  local copies, waits for them, and re-layouts  31.1 us (10%)
  matrix products  22.7 us (7%)
  between operations  13.4 us (4%)
  starting transfers between devices  11.9 us (4%)
    reduce_scatter x1, waiting for transfers between devices, shards(): return lax.psum_scatter(part, 'dp', scatter_dimension=1, tiled=True)  157 us
    all_to_all x1, waiting for transfers between devices, shards(): xg = jnp.concatenate(lax.all_to_all(outgoing, 'expert', 0, 0), axis=0)  89.8 us
    dot_general x1, matrix products, shards(): jnp.einsum('eth,tf->ehf', xm, dyg, preferred_element_type=jnp.float32)  22.7 us
    mul x2, local copies, waits for them, and re-layouts, shards(): xm = xg[None] * mask[:, :, None]  11.9 us
    all_to_all x1, local copies, waits for them, and re-layouts, shards(): xg = jnp.concatenate(lax.all_to_all(outgoing, 'expert', 0, 0), axis=0)  11.4 us
    all_to_all x1, starting transfers between devices, shards(): xg = jnp.concatenate(lax.all_to_all(outgoing, 'expert', 0, 0), axis=0)  7.12 us
  transfers between devices with their start and end apart: 3, of which 3 were waited for; matrix products, arithmetic and copies ran while one was open for 8% of the time, Pallas kernels for 0%

profile of v1, /device:TPU:8, one launch (start us, length us, event | category | flops | bytes accessed | tf_op | source)
XLA Modules:
  0.0 326.6 jit_solution(7291848962680760954)
XLA Ops:
  6.5 1.5 copy.18
  8.0 3.9 %stack.2 = bf16[8,512,1024]{1,2,0:T(8,128)(2,1)} broadcast(bf16[512,1024]{0,1:T(8,128)(2,1)S(1)} %copy.18), dimensions={1,2} | broadcast | bytes 9437184 | tf_op jit(solution)/shard_map/stack | solution.py:26
  12.0 0.0 copy-start
  12.0 7.1 %all-to-all-start = ((bf16[8,512,1024]{1,2,0:T(8,128)(2,1)}), bf16[8,512,1024]{1,2,0:T(8,128)(2,1)}, u32[]{:S(2)}, u32[]{:S(2)}) async-start(bf16[8,512,1024]{1,2,0:T(8,128)(2,1)} %stack.2), calls=%async_computation | async-start | bytes 16777216 | tf_op jit(solution)/shard_map/all_to_all | solution.py:27
  19.1 0.0 copy-done
  19.1 1.5 copy.26
  20.6 89.8 %all-to-all-done = bf16[8,512,1024]{1,2,0:T(8,128)(2,1)} async-done(((bf16[8,512,1024]{1,2,0:T(8,128)(2,1)}), bf16[8,512,1024]{1,2,0:T(8,128)(2,1)}, u32[]{:S(2)}, u32[]{:S(2)}) %all-to-all-start) | async-done | bytes 8388640 | tf_op jit(solution)/shard_map/all_to_all | solution.py:27
  110.3 4.8 %all-to-all-start.1 = ((bf16[512,8,256]{2,0,1:T(8,128)(2,1)}), bf16[512,8,256]{2,0,1:T(8,128)(2,1)S(1)}, u32[]{:S(2)}, u32[]{:S(2)}) async-start(bf16[512,8,256]{2,0,1:T(8,128)(2,1)} %bitcast.14), calls=%async_computation.1 | async-start | bytes 4194304 | tf_op jit(solution)/shard_map/all_to_all | solution.py:28
  115.1 0.0 reduce-scatter.2.cloned.1.call-start
  115.1 0.0 copy-done.1
  115.1 0.1 copy.21
  115.3 0.6 gather_fusion
  115.9 0.2 reduce_window_sum.11
  116.0 0.1 convert_reduce_fusion
  116.2 0.1 copy.22
  116.2 0.1 eq.15
  116.3 0.1 fusion.4
  116.4 0.1 broadcast_bitcast_fusion
  116.5 11.4 %copy.19 = bf16[8,512,1024]{2,1,0:T(8,128)(2,1)} copy(bf16[8,512,1024]{1,2,0:T(8,128)(2,1)} %all-to-all-done) | data formatting | bytes 16777216 | tf_op jit(solution)/shard_map/all_to_all | solution.py:27
  128.0 11.8 %copy.20 = bf16[4096,1024]{0,1:T(8,128)(2,1)} copy(bf16[4096,1024]{1,0:T(8,128)(2,1)} %bitcast.15) | data formatting | bytes 16777216 | tf_op jit(solution)/shard_map/mul | solution.py:29
  139.8 0.4 all-to-all-done.1
  140.2 22.7 %fusion = f32[8,1024,256]{2,1,0:T(8,128)} fusion(bf16[4096,256,1]{1,0,2:T(8,128)(2,1)S(1)} %bitcast.17, bf16[8,4096]{1,0:T(8,128)(2,1)S(1)} %broadcast_bitcast_fusion, bf16[4096,1024]{0,1:T(8,128)(2,1)} %copy.20), kind=kOutput, calls=%fused_computation.1 | convolution fusion | flops 17213423616 | bytes 18939904 | tf_op jit(solution)/shard_map/eth,tf->ehf/dot_general | solution.py:30
  162.9 0.0 reduce-scatter.2.cloned.1.call-update
  162.9 156.8 %reduce-scatter.2.cloned.1.call-done = f32[8,32,256]{2,1,0:T(8,128)} async-done(((f32[8,1024,256]{2,1,0:T(8,128)}), f32[8,32,256]{2,1,0:T(8,128)}) %reduce-scatter.2.cloned.1.call-update) | async-done | bytes 262160 | tf_op jit(solution)/shard_map/reduce_scatter | solution.py:31
  (3 shorter events, 0.0 us)
Async XLA Ops:
  12.0 7.1 %copy-start = (bf16[512,2048]{1,0:T(8,128)(2,1)S(1)}, bf16[512,2048]{1,0:T(8,128)(2,1)}, u32[]{:S(2)}) copy-start(bf16[512,2048]{1,0:T(8,128)(2,1)} %param.4) | copy-start | bytes 6291460
  12.0 98.4 %all-to-all-start = ((bf16[8,512,1024]{1,2,0:T(8,128)(2,1)}), bf16[8,512,1024]{1,2,0:T(8,128)(2,1)}, u32[]{:S(2)}, u32[]{:S(2)}) async-start(bf16[8,512,1024]{1,2,0:T(8,128)(2,1)} %stack.2), calls=%async_computation | async-start | bytes 16777216 | tf_op jit(solution)/shard_map/all_to_all | solution.py:27
  19.1 96.0 %copy-start.1 = (s32[256,8]{0,1:T(8,128)S(1)}, s32[256,8]{0,1:T(8,128)}, u32[]{:S(2)}) copy-start(s32[256,8]{0,1:T(8,128)} %param.5) | copy-start | bytes 24580
  110.3 29.9 %all-to-all-start.1 = ((bf16[512,8,256]{2,0,1:T(8,128)(2,1)}), bf16[512,8,256]{2,0,1:T(8,128)(2,1)S(1)}, u32[]{:S(2)}, u32[]{:S(2)}) async-start(bf16[512,8,256]{2,0,1:T(8,128)(2,1)} %bitcast.14), calls=%async_computation.1 | async-start | bytes 4194304 | tf_op jit(solution)/shard_map/all_to_all | solution.py:28
  115.1 204.6 %reduce-scatter.2.cloned.1.call-start = ((), (), s32[]{:S(2)}) async-start(), calls=%async_computation.3 | async-start | bytes 8650752 | tf_op jit(solution)/shard_map/reduce_scatter | solution.py:31
Sparse Core Ops, SparseCore 0:
  163.1 156.6 reduce-scatter.1
